TPU v7x, 32 devices: a whole 2x2x4 slice. The times are simulated.
32 devices in a mesh: blk: 8 (over y, x, core), layer: 4 (over z).
Axes of the slice: x: 2, y: 2, z: 4, core: 2. Of those that a mesh axis runs over, the one named last changes fastest.
Arguments:
- points: float32 [8192, 128], P('blk'), may hold values from -6 to 6
- inv_scale: float32 [128], replicated, may hold values from 0.01 to 0.25
- vectors: float32 [8192, 64], P('blk'), may hold values from -6 to 6
- noise: float32 [8192], P(('blk', 'layer')), may hold values from 0.1 to 1
Outputs:
- result: float32 [8192, 64], P(('blk', 'layer'))
All inputs are finite; a program needn't handle non-finite values.
Results may differ from a plain program's by a relative error of at most 0.0001.
Values sent between devices are 32-bit elements; how exact they have to be, the bound alone decides.
A program may use at most 64 MiB of HBM per device.

v0:
```python
import functools
import math

import jax
import jax.numpy as jnp
from jax import lax
from jax.experimental import pallas as pl
from jax.experimental.pallas import tpu as pltpu
from jax.sharding import PartitionSpec as P

MESH = pl.DeviceIdType.MESH
LOG2 = math.log(2.0)
UNIT = math.sqrt(5.0) / LOG2
BF16 = jnp.bfloat16
F32 = jnp.float32


def two_terms(value):
    high = value.astype(BF16).astype(F32)
    return high, (value - high).astype(BF16).astype(F32)


def augmented(points, scale, left):
    high, low = two_terms(points * scale)
    held = high + low
    norm = jnp.sum(held * held, axis=1, keepdims=True)
    first = norm.astype(BF16).astype(F32)
    second = (norm - first).astype(BF16).astype(F32)
    third = norm - first - second
    lane = lax.broadcasted_iota(jnp.int32, high.shape, 1)
    at, ones = (0, 3) if left else (3, 0)
    extra = jnp.where(
        lane == at,
        first,
        jnp.where(
            lane == at + 1,
            second,
            jnp.where(
                lane == at + 2,
                third,
                jnp.where((lane >= ones) & (lane < ones + 3), 1.0, 0.0),
            ),
        ),
    )
    if left:
        high, low = -2.0 * high, -2.0 * low
        terms = (high, high, low, extra)
    else:
        terms = (high, low, high, extra)
    return jnp.concatenate([term.astype(BF16) for term in terms], axis=1)


def nt_dot(left, right):
    return lax.dot_general(left, right, (((1,), (1,)), ((), ())), preferred_element_type=F32)


def kernel(
    blocks, layers, tile, points, scale, vectors, noise, out,
    p_own, v_own, p_in, v_in, left, v_left, direct, m_out, d_out, m_in, d_in,
    own_sem, p_send, v_send, p_recv, v_recv, pf_send, vf_send, m_send, m_recv, d_send, d_recv,
):
    block, layer = lax.axis_index("blk"), lax.axis_index("layer")
    core = lax.rem(block, 2)
    sibling = block + 1 - 2 * core
    rows, columns = p_own.shape[0], v_own.shape[0]
    piece = rows // layers

    def wrapped(index):
        return lax.rem(index + 2 * blocks, blocks)

    first_core = block - core
    partner = jnp.where(
        layer == 0,
        block,
        jnp.where(
            layer == 1,
            jnp.where(core == 0, block + 1, wrapped(block + layers - 1)),
            wrapped(first_core + layer),
        ),
    )
    shares = layer >= 2
    spreads = shares & (core == lax.rem(layer, 2))
    sends = (layer == 1) | spreads

    own_p = pltpu.make_async_copy(points, p_own, own_sem.at[0])
    own_v = pltpu.make_async_copy(vectors, v_own, own_sem.at[1])
    own_p.start()
    own_v.start()

    @pl.when(layer == 0)
    def _():
        for c in range(layers):
            at = pl.ds(c * piece, piece)
            pltpu.make_async_copy(points.at[at], p_in.at[c], p_recv.at[c]).start()
            pltpu.make_async_copy(vectors.at[:, at], v_in.at[c], v_recv.at[c]).start()

    barrier = pltpu.get_barrier_semaphore()

    def greet(to_block, to_layer):
        pl.semaphore_signal(barrier, inc=1, device_id=(to_block, to_layer), device_id_type=MESH)

    @pl.when(layer == 1)
    def _():
        greet(partner, layer)

    @pl.when(shares)
    def _():
        greet(partner, layer)
        greet(sibling, layer)

    for other in range(layers):

        @pl.when(layer != other)
        def _():
            greet(block, other)

    greet(wrapped(jnp.where(core == 1, block - 1, block - (layers - 1))), 1)
    for other in range(2, layers):

        @pl.when(core == other % 2)
        def _():
            greet(wrapped(block - other), other)
            greet(wrapped(block - other + 1), other)

    expected = layers - 1
    expected += jnp.where(layer >= 1, layers, 0) + jnp.where(sends, 1, 0)
    expected += jnp.where(shares, 1, 0) + jnp.where(spreads, 1, 0)
    pl.semaphore_wait(barrier, expected)

    own_p.wait()
    own_v.wait()

    def far(c):
        at = pl.ds(c * piece, piece)
        target = wrapped(
            jnp.where(
                layer == 1,
                jnp.where(core == 1, block - 1, block - (layers - 1)),
                block - layer + c % 2,
            )
        )
        return (
            pltpu.make_async_remote_copy(
                p_own.at[at], p_in.at[c], p_send.at[c], p_recv.at[c], (target, layer), MESH
            ),
            pltpu.make_async_remote_copy(
                v_own.at[:, at], v_in.at[c], v_send.at[c], v_recv.at[c], (target, layer), MESH
            ),
        )

    def near(c):
        return (
            pltpu.make_async_remote_copy(
                p_in.at[c], p_in.at[c], pf_send.at[c], p_recv.at[c], (sibling, layer), MESH
            ),
            pltpu.make_async_remote_copy(
                v_in.at[c], v_in.at[c], vf_send.at[c], v_recv.at[c], (sibling, layer), MESH
            ),
        )

    slot = jnp.where(layer == 1, 0, 1 + 2 * (layer // 2 - 1) + core)

    def mirrored_copy(c):
        return pltpu.make_async_remote_copy(
            m_out.at[c], m_in.at[slot], m_send.at[c], m_recv.at[slot], (partner, c), MESH
        )

    def direct_copy(c):
        return pltpu.make_async_remote_copy(
            d_out.at[c], d_in.at[layer], d_send.at[c], d_recv.at[layer], (block, c), MESH
        )

    @pl.when(sends)
    def _():
        for c in range(layers):
            for copy in far(c):
                copy.start()

    unit = scale[...] * UNIT
    left[...] = augmented(p_own[...], unit, True)
    v_left[...] = jnp.concatenate(two_terms(v_own[...]), axis=0).astype(BF16)

    for c in range(layers):
        pltpu.make_async_copy(p_in.at[c], p_in.at[c], p_recv.at[c]).wait()
        pltpu.make_async_copy(v_in.at[c], v_in.at[c], v_recv.at[c]).wait()

        @pl.when(shares & (core == c % 2))
        def _():
            for copy in near(c):
                copy.start()

        right = augmented(p_in[c], unit, False)
        v_right = jnp.concatenate(two_terms(v_in[c]), axis=0).T.astype(BF16)
        mirrored = None
        for start in range(0, rows, tile):
            at = pl.ds(start, tile)
            square = jnp.maximum(nt_dot(left[at, :], right), 1e-20)
            u = square * lax.rsqrt(square)
            value = (1.0 + u * (LOG2 + u * (LOG2 * LOG2 / 3.0))) * jnp.exp2(-u)
            high = value.astype(BF16)
            low = (value - high.astype(F32)).astype(BF16)
            term = jnp.dot(high, v_right, preferred_element_type=F32)
            term += jnp.dot(low, v_right, preferred_element_type=F32)
            if c == 0:
                direct[at, :] = term
            else:
                direct[at, :] += term
            turned = jnp.dot(v_left[:, at], high, preferred_element_type=F32)
            turned += jnp.dot(v_left[:, at], low, preferred_element_type=F32)
            mirrored = turned if mirrored is None else mirrored + turned
        m_out[c] = mirrored[:columns] + mirrored[columns:]

        @pl.when(layer >= 1)
        def _():
            mirrored_copy(c).start()

    for c in range(layers):
        turned = direct[pl.ds(c * piece, piece), :].T
        turned = turned[:columns] + turned[columns:]

        @pl.when(layer == c)
        def _():
            d_in[c] = turned

        @pl.when(layer != c)
        def _():
            d_out[c] = turned
            direct_copy(c).start()

    for s in range(layers - 1):
        pltpu.make_async_copy(m_in.at[s], m_in.at[s], m_recv.at[s]).wait()
    total = m_in[0]
    for s in range(1, layers - 1):
        total += m_in[s]
    for s in range(layers):

        @pl.when(layer != s)
        def _():
            pltpu.make_async_copy(d_in.at[s], d_in.at[s], d_recv.at[s]).wait()

    for s in range(layers):
        total += d_in[s]
    mine = v_own[:, pl.ds(pl.multiple_of(layer * piece, 128), piece)]
    normalizer = float(rows * (2 * layers - 1)) ** (-0.5)
    out[...] = total * normalizer + noise[...] * mine

    @pl.when(sends)
    def _():
        for c in range(layers):
            for copy in far(c):
                copy.wait_send()

    for c in range(layers):

        @pl.when(shares & (core == c % 2))
        def _():
            for copy in near(c):
                copy.wait_send()

        @pl.when(layer >= 1)
        def _():
            mirrored_copy(c).wait_send()

        @pl.when(layer != c)
        def _():
            direct_copy(c).wait_send()


def per_device(points, inv_scale, vectors, noise):
    blocks, layers = lax.axis_size("blk"), lax.axis_size("layer")
    rows, features = points.shape
    columns = vectors.shape[1]
    piece = rows // layers
    tile = min(256, rows)
    vmem = pl.BlockSpec(memory_space=pltpu.VMEM)
    hbm = pl.BlockSpec(memory_space=pl.ANY)
    dma = pltpu.SemaphoreType.DMA
    out = pl.pallas_call(
        functools.partial(kernel, blocks, layers, tile),
        out_shape=jax.ShapeDtypeStruct((columns, piece), F32),
        in_specs=[hbm, vmem, hbm, vmem],
        out_specs=vmem,
        scratch_shapes=[
            pltpu.VMEM((rows, features), F32),
            pltpu.VMEM((columns, rows), F32),
            pltpu.VMEM((layers, piece, features), F32),
            pltpu.VMEM((layers, columns, piece), F32),
            pltpu.VMEM((rows, 4 * features), BF16),
            pltpu.VMEM((2 * columns, rows), BF16),
            pltpu.VMEM((rows, 2 * columns), F32),
            pltpu.VMEM((layers, columns, piece), F32),
            pltpu.VMEM((layers, columns, piece), F32),
            pltpu.VMEM((layers - 1, columns, piece), F32),
            pltpu.VMEM((layers, columns, piece), F32),
            dma((2,)),
            *[dma((layers,)) for _ in range(7)],
            dma((layers - 1,)),
            dma((layers,)),
            dma((layers,)),
        ],
        compiler_params=pltpu.CompilerParams(collective_id=0, has_side_effects=True),
    )(points, inv_scale[None, :], vectors.T, noise[None, :])
    return out.T


def solution(mesh):
    placed = (P("blk", None), P(), P("blk", None), P(("blk", "layer")))
    return jax.shard_map(
        per_device, mesh=mesh, in_specs=placed, out_specs=P(("blk", "layer"), None), check_vma=False
    )
```

profile of v0, /device:TPU:0, one launch (start us, length us, event | category | flops | bytes accessed | tf_op | source)
XLA Modules:
  0.0 29.1 jit_solution(10952569165036293030)
XLA Ops:
  0.0 27.6 %shard_map.46 = f32[64,256]{1,0:T(8,128)} custom-call(f32[1024,128]{1,0:T(8,128)} %points.1, f32[1,128]{1,0:T(1,128)} %bitcast.7, f32[64,1024]{1,0:T(8,128)} %bitcast.5, f32[1,256]{1,0:T(1,128)} %bitcast.6), custom_call_target="tpu_custom_call" | custom-call | tf_op jit(solution)/shard_map/pallas_call | solution.py:278
  27.6 1.5 %copy.6 = f32[256,64]{0,1:T(8,128)} copy(f32[256,64]{0,1:T(8,128)} %bitcast.4) | data formatting | bytes 131072
where the time goes:
time: 29.2 us; the launch traced here: 29.1 us
  Pallas kernels  27.6 us (95%)
  local copies, waits for them, and re-layouts  1.47 us (5%)
    pallas_call x1, Pallas kernels, per_device(): pl.pallas_call(functools.partial(kernel, blocks, layers, tile), out_shape...  27.6 us
    unnamed x1, local copies, waits for them, and re-layouts  1.47 us

commit v1 on v0

v1 whole, which is shorter than its diff:
```python
import functools
import math

import jax
import jax.numpy as jnp
from jax import lax
from jax.experimental import pallas as pl
from jax.experimental.pallas import tpu as pltpu
from jax.sharding import PartitionSpec as P

MESH = pl.DeviceIdType.MESH
LOG2 = math.log(2.0)
UNIT = math.sqrt(5.0) / LOG2
SHIFT = 1.5 / LOG2
REST = 3.0 / LOG2**2 - SHIFT**2
GAIN = LOG2**2 / 3.0 * 2.0**SHIFT
BF16 = jnp.bfloat16
F32 = jnp.float32


def two_terms(value):
    high = value.astype(BF16).astype(F32)
    return high, (value - high).astype(BF16).astype(F32)


def augmented(points, scale, left):
    high, low = two_terms(points * scale)
    held = high + low
    norm = jnp.sum(held * held, axis=1, keepdims=True)
    first = norm.astype(BF16).astype(F32)
    second = (norm - first).astype(BF16).astype(F32)
    third = norm - first - second
    lane = lax.broadcasted_iota(jnp.int32, high.shape, 1)
    at, ones = (0, 3) if left else (3, 0)
    extra = jnp.where(
        lane == at,
        first,
        jnp.where(
            lane == at + 1,
            second,
            jnp.where(
                lane == at + 2,
                third,
                jnp.where((lane >= ones) & (lane < ones + 3), 1.0, 0.0),
            ),
        ),
    )
    if left:
        high, low = -2.0 * high, -2.0 * low
        terms = (high, high, low, extra)
    else:
        terms = (high, low, high, extra)
    return jnp.concatenate([term.astype(BF16) for term in terms], axis=1)


def nt_dot(left, right):
    return lax.dot_general(left, right, (((1,), (1,)), ((), ())), preferred_element_type=F32)


def kernel(
    chips, layers, tile, points, scale, vectors, noise, out,
    p_data, v_data, s_data, n_data, q_in, left, v_left, right, high, low, r_out, r_in,
    own_sem, p_send, p_recv, v_send, v_recv, q_send, q_recv, r_send, r_recv,
):
    block, layer = lax.axis_index("blk"), lax.axis_index("layer")
    core = lax.rem(block, 2)
    chip = block // 2
    rows, columns = p_data.shape[1], v_data.shape[1]
    piece = rows // layers
    mine = pl.ds(pl.multiple_of(layer * piece, piece), piece)
    sibling = (block + 1 - 2 * core, layer)
    others = range(1, chips)

    def peer(i):
        return (2 * (chip ^ i) + core, layer)

    barrier = pltpu.get_barrier_semaphore()
    for target in (*(peer(i) for i in others), sibling):
        pl.semaphore_signal(barrier, inc=1, device_id=target, device_id_type=MESH)

    own = (
        pltpu.make_async_copy(points, p_data.at[0], own_sem.at[0]),
        pltpu.make_async_copy(scale, s_data, own_sem.at[1]),
        pltpu.make_async_copy(vectors, v_data.at[0], own_sem.at[2]),
        pltpu.make_async_copy(noise, n_data, own_sem.at[3]),
    )
    for copy in own:
        copy.start()

    def query(i):
        return pltpu.make_async_remote_copy(
            p_data.at[0, mine], q_in.at[i - 1], q_send.at[i - 1], q_recv.at[i - 1], peer(i), MESH
        )

    def result(i):
        return pltpu.make_async_remote_copy(
            r_out.at[i - 1], r_in.at[i - 1], r_send.at[i - 1], r_recv.at[i - 1], peer(i), MESH
        )

    across = (
        pltpu.make_async_remote_copy(p_data.at[0], p_data.at[1], p_send, p_recv, sibling, MESH),
        pltpu.make_async_remote_copy(v_data.at[0], v_data.at[1], v_send, v_recv, sibling, MESH),
    )

    for copy in own:
        copy.wait()
    pl.semaphore_wait(barrier, chips)
    for i in others:
        query(i).start()
    for copy in across:
        copy.start()

    unit = s_data[...] * UNIT

    def prepare(slot):
        left[slot] = augmented(p_data[slot], unit, True)
        v_left[slot] = jnp.concatenate(two_terms(v_data[slot]), axis=0).astype(BF16)

    def product(slot):
        for start in range(0, rows, tile):
            at = pl.ds(start, tile)
            square = jnp.maximum(nt_dot(left[slot, at, :], right[...]), 1e-20)
            z = -SHIFT - square * lax.rsqrt(square)
            value = (z * z + REST) * jnp.exp2(z)
            high[at, :] = value.astype(BF16)
            low[at, :] = (value - value.astype(BF16).astype(F32)).astype(BF16)
        turned = jnp.dot(v_left[slot], high[...], preferred_element_type=F32)
        turned_low = jnp.dot(v_left[slot, :columns], low[...], preferred_element_type=F32)
        return turned[:columns] + turned[columns:] + turned_low

    prepare(0)
    right[...] = augmented(p_data[0, mine], unit, False)
    total = product(0)
    for copy in across:
        copy.wait()
    prepare(1)
    total += product(1)

    for i in others:
        query(i).wait()
        right[...] = augmented(q_in[i - 1], unit, False)
        partial = product(1)
        if 2 * i != chips:
            partial += product(0)
        r_out[i - 1] = partial
        result(i).start()

    for i in others:
        result(i).wait()
        total += r_in[i - 1]
    normalizer = GAIN * float(rows * (2 * layers - 1)) ** (-0.5)
    held = v_data[0, :, pl.ds(pl.multiple_of(layer * piece, 128), piece)]
    out[...] = total * normalizer + n_data[...] * held


def per_device(points, inv_scale, vectors, noise):
    blocks, layers = lax.axis_size("blk"), lax.axis_size("layer")
    chips = blocks // 2
    rows, features = points.shape
    columns = vectors.shape[1]
    piece = rows // layers
    assert blocks == 2 * layers and chips & (chips - 1) == 0
    tile = min(256, rows)
    hbm = pl.BlockSpec(memory_space=pl.ANY)
    dma = pltpu.SemaphoreType.DMA
    peers = chips - 1
    out = pl.pallas_call(
        functools.partial(kernel, chips, layers, tile),
        out_shape=pltpu.VMEM((columns, piece), F32),
        in_specs=[hbm] * 4,
        out_specs=pl.BlockSpec(memory_space=pltpu.VMEM),
        scratch_shapes=[
            pltpu.VMEM((2, rows, features), F32),
            pltpu.VMEM((2, columns, rows), F32),
            pltpu.VMEM((1, features), F32),
            pltpu.VMEM((1, piece), F32),
            pltpu.VMEM((peers, piece, features), F32),
            pltpu.VMEM((2, rows, 4 * features), BF16),
            pltpu.VMEM((2, 2 * columns, rows), BF16),
            pltpu.VMEM((piece, 4 * features), BF16),
            pltpu.VMEM((rows, piece), BF16),
            pltpu.VMEM((rows, piece), BF16),
            pltpu.VMEM((peers, columns, piece), F32),
            pltpu.VMEM((peers, columns, piece), F32),
            dma((4,)),
            *[dma(()) for _ in range(4)],
            *[dma((peers,)) for _ in range(4)],
        ],
        compiler_params=pltpu.CompilerParams(collective_id=0, has_side_effects=True),
    )(points, inv_scale[None, :], vectors.T, noise[None, :])
    return out.T


def solution(mesh):
    placed = (P("blk", None), P(), P("blk", None), P(("blk", "layer")))
    return jax.shard_map(
        per_device, mesh=mesh, in_specs=placed, out_specs=P(("blk", "layer"), None), check_vma=False
    )
```

time: 29.2 us -> 17.9 us (0.61)
  Pallas kernels: 27.6 us -> 17.1 us
  local copies, waits for them, and re-layouts: 1.47 us -> 0.63 us
    pallas_call x1, Pallas kernels: 27.6 us -> 17.1 us  [per_device(): pl.pallas_call(functools.partial(kernel, chips, layers, tile), out_shape=...]
    unnamed x1, local copies, waits for them, and re-layouts: 1.47 us -> 0.63 us
where the time goes in v1:
time: 17.9 us; the launch traced here: 17.7 us
  Pallas kernels  17.1 us (96%)
  local copies, waits for them, and re-layouts  0.63 us (4%)
    pallas_call x1, Pallas kernels, per_device(): pl.pallas_call(functools.partial(kernel, chips, layers, tile), out_shape=...  17.1 us
    unnamed x1, local copies, waits for them, and re-layouts  0.63 us

profile of v1, /device:TPU:0, one launch (start us, length us, event | category | flops | bytes accessed | tf_op | source)
XLA Modules:
  0.0 17.7 jit_solution(2990407580404022154)
XLA Ops:
  0.0 17.1 %shard_map.46 = f32[64,256]{1,0:T(8,128)S(1)} custom-call(f32[1024,128]{1,0:T(8,128)} %points.1, f32[1,128]{1,0:T(1,128)} %bitcast.7, f32[64,1024]{1,0:T(8,128)} %bitcast.5, f32[1,256]{1,0:T(1,128)} %bitcast.6), custom_call_target="tpu_custom_call" | custom-call | tf_op jit(solution)/shard_map/pallas_call | solution.py:167
  17.1 0.6 %copy.6 = f32[256,64]{0,1:T(8,128)} copy(f32[256,64]{0,1:T(8,128)S(1)} %bitcast.4) | data formatting | bytes 131072

commit v2 on v1

--- a/solution.py
+++ b/solution.py
@@ -70,12 +70,14 @@
     mine = pl.ds(pl.multiple_of(layer * piece, piece), piece)
     sibling = (block + 1 - 2 * core, layer)
     others = range(1, chips)
+    bits = [1 << d for d in range(chips.bit_length() - 1)]
+    half = piece // 2
 
     def peer(i):
         return (2 * (chip ^ i) + core, layer)
 
     barrier = pltpu.get_barrier_semaphore()
-    for target in (*(peer(i) for i in others), sibling):
+    for target in (*(peer(bit) for bit in bits), sibling):
         pl.semaphore_signal(barrier, inc=1, device_id=target, device_id_type=MESH)
 
     own = (
@@ -87,10 +89,29 @@
     for copy in own:
         copy.start()
 
-    def query(i):
+    def last_bit(i, h):
+        return i & -i if h else 1 << (i.bit_length() - 1)
+
+    def nth(i, turn):
+        return turn if i * i < chips else 1 - turn
+
+    def query(i, h):
+        bit = last_bit(i, h)
+        before = i ^ bit
+        at = pl.ds(pl.multiple_of(layer * piece + h * half, half), half)
         return pltpu.make_async_remote_copy(
-            p_data.at[0, mine], q_in.at[i - 1], q_send.at[i - 1], q_recv.at[i - 1], peer(i), MESH
+            q_in.at[before - 1, h] if before else p_data.at[0, at],
+            q_in.at[i - 1, h],
+            q_send.at[i - 1, h],
+            q_recv.at[i - 1, h],
+            peer(bit),
+            MESH,
         )
+
+    def relay(i, h):
+        for j in others:
+            if j ^ last_bit(j, h) == i:
+                query(j, h).start()
 
     def result(i):
         return pltpu.make_async_remote_copy(
@@ -104,12 +125,6 @@
 
     for copy in own:
         copy.wait()
-    pl.semaphore_wait(barrier, chips)
-    for i in others:
-        query(i).start()
-    for copy in across:
-        copy.start()
-
     unit = s_data[...] * UNIT
 
     def prepare(slot):
@@ -130,22 +145,37 @@
 
     prepare(0)
     right[...] = augmented(p_data[0, mine], unit, False)
+    pl.semaphore_wait(barrier, 1 + len(bits))
+    for turn in (0, 1):
+        for bit in bits:
+            query(bit, nth(bit, turn)).start()
+    for copy in across:
+        copy.start()
     total = product(0)
     for copy in across:
         copy.wait()
     prepare(1)
     total += product(1)
 
+    for count in range(1, len(bits) + 1):
+        level = [i for i in others if i.bit_count() == count]
+        for i in level:
+            query(i, nth(i, 0)).wait_recv()
+            relay(i, nth(i, 0))
+        for i in level:
+            query(i, nth(i, 1)).wait_recv()
+            relay(i, nth(i, 1))
+            both = jnp.concatenate([q_in[i - 1, 0], q_in[i - 1, 1]], axis=0)
+            right[...] = augmented(both, unit, False)
+            partial = product(1)
+            if 2 * i != chips:
+                partial += product(0)
+            r_out[i - 1] = partial
+            result(i).start()
+
     for i in others:
-        query(i).wait()
-        right[...] = augmented(q_in[i - 1], unit, False)
-        partial = product(1)
-        if 2 * i != chips:
-            partial += product(0)
-        r_out[i - 1] = partial
-        result(i).start()
-
-    for i in others:
+        for h in (0, 1):
+            query(i, h).wait_send()
         result(i).wait()
         total += r_in[i - 1]
     normalizer = GAIN * float(rows * (2 * layers - 1)) ** (-0.5)
@@ -174,7 +204,7 @@
             pltpu.VMEM((2, columns, rows), F32),
             pltpu.VMEM((1, features), F32),
             pltpu.VMEM((1, piece), F32),
-            pltpu.VMEM((peers, piece, features), F32),
+            pltpu.VMEM((peers, 2, piece // 2, features), F32),
             pltpu.VMEM((2, rows, 4 * features), BF16),
             pltpu.VMEM((2, 2 * columns, rows), BF16),
             pltpu.VMEM((piece, 4 * features), BF16),
@@ -184,7 +214,8 @@
             pltpu.VMEM((peers, columns, piece), F32),
             dma((4,)),
             *[dma(()) for _ in range(4)],
-            *[dma((peers,)) for _ in range(4)],
+            *[dma((peers, 2)) for _ in range(2)],
+            *[dma((peers,)) for _ in range(2)],
         ],
         compiler_params=pltpu.CompilerParams(collective_id=0, has_side_effects=True),
     )(points, inv_scale[None, :], vectors.T, noise[None, :])

time: 17.9 us -> 18.1 us (1.011)
  Pallas kernels: 17.1 us -> 17.3 us
    pallas_call x1, Pallas kernels: 17.1 us -> 17.3 us  [per_device(): pl.pallas_call(functools.partial(kernel, chips, layers, tile), out_shape=...]
where the time goes in v2:
time: 18.1 us; the launch traced here: 17.9 us
  Pallas kernels  17.3 us (96%)
  local copies, waits for them, and re-layouts  0.63 us (3%)
    pallas_call x1, Pallas kernels, per_device(): pl.pallas_call(functools.partial(kernel, chips, layers, tile), out_shape=...  17.3 us
    unnamed x1, local copies, waits for them, and re-layouts  0.63 us

profile of v2, /device:TPU:0, one launch (start us, length us, event | category | flops | bytes accessed | tf_op | source)
XLA Modules:
  0.0 17.9 jit_solution(1191254257259323566)
XLA Ops:
  0.0 17.3 %shard_map.46 = f32[64,256]{1,0:T(8,128)S(1)} custom-call(f32[1024,128]{1,0:T(8,128)} %points.1, f32[1,128]{1,0:T(1,128)} %bitcast.7, f32[64,1024]{1,0:T(8,128)} %bitcast.5, f32[1,256]{1,0:T(1,128)} %bitcast.6), custom_call_target="tpu_custom_call" | custom-call | tf_op jit(solution)/shard_map/pallas_call | solution.py:197
  17.3 0.6 %copy.6 = f32[256,64]{0,1:T(8,128)} copy(f32[256,64]{0,1:T(8,128)S(1)} %bitcast.4) | data formatting | bytes 131072

commit v3 on v2

--- a/solution.py
+++ b/solution.py
@@ -58,7 +58,7 @@
 
 
 def kernel(
-    chips, layers, tile, points, scale, vectors, noise, out,
+    chips, layers, parts, tile, points, scale, vectors, noise, out,
     p_data, v_data, s_data, n_data, q_in, left, v_left, right, high, low, r_out, r_in,
     own_sem, p_send, p_recv, v_send, v_recv, q_send, q_recv, r_send, r_recv,
 ):
@@ -71,13 +71,13 @@
     sibling = (block + 1 - 2 * core, layer)
     others = range(1, chips)
     bits = [1 << d for d in range(chips.bit_length() - 1)]
-    half = piece // 2
-
-    def peer(i):
-        return (2 * (chip ^ i) + core, layer)
+    part = piece // parts
+
+    def peer(i, same=False):
+        return (2 * (chip ^ i) + (core if same else 1 - core), layer)
 
     barrier = pltpu.get_barrier_semaphore()
-    for target in (*(peer(bit) for bit in bits), sibling):
+    for target in (*(peer(bit, same) for bit in bits for same in (False, True)), sibling):
         pl.semaphore_signal(barrier, inc=1, device_id=target, device_id_type=MESH)
 
     own = (
@@ -90,21 +90,21 @@
         copy.start()
 
     def last_bit(i, h):
-        return i & -i if h else 1 << (i.bit_length() - 1)
+        return i & -i if 2 * h >= parts else 1 << (i.bit_length() - 1)
 
     def nth(i, turn):
-        return turn if i * i < chips else 1 - turn
+        return turn if i * i < chips else (turn + parts // 2) % parts
 
     def query(i, h):
         bit = last_bit(i, h)
         before = i ^ bit
-        at = pl.ds(pl.multiple_of(layer * piece + h * half, half), half)
+        at = pl.ds(pl.multiple_of(layer * piece + h * part, part), part)
         return pltpu.make_async_remote_copy(
             q_in.at[before - 1, h] if before else p_data.at[0, at],
             q_in.at[i - 1, h],
             q_send.at[i - 1, h],
             q_recv.at[i - 1, h],
-            peer(bit),
+            peer(bit, same=before > 0),
             MESH,
         )
 
@@ -131,50 +131,83 @@
         left[slot] = augmented(p_data[slot], unit, True)
         v_left[slot] = jnp.concatenate(two_terms(v_data[slot]), axis=0).astype(BF16)
 
-    def product(slot):
+    def evaluate(queries, slot, buffer):
         for start in range(0, rows, tile):
             at = pl.ds(start, tile)
-            square = jnp.maximum(nt_dot(left[slot, at, :], right[...]), 1e-20)
+            square = jnp.maximum(nt_dot(left[slot, at, :], queries), 1e-20)
             z = -SHIFT - square * lax.rsqrt(square)
             value = (z * z + REST) * jnp.exp2(z)
-            high[at, :] = value.astype(BF16)
-            low[at, :] = (value - value.astype(BF16).astype(F32)).astype(BF16)
-        turned = jnp.dot(v_left[slot], high[...], preferred_element_type=F32)
-        turned_low = jnp.dot(v_left[slot, :columns], low[...], preferred_element_type=F32)
+            high[buffer, at, :] = value.astype(BF16)
+            low[buffer, at, :] = (value - value.astype(BF16).astype(F32)).astype(BF16)
+
+    def product(slot, buffer):
+        turned = jnp.dot(v_left[slot], high[buffer], preferred_element_type=F32)
+        turned_low = jnp.dot(v_left[slot, :columns], low[buffer], preferred_element_type=F32)
         return turned[:columns] + turned[columns:] + turned_low
 
-    prepare(0)
-    right[...] = augmented(p_data[0, mine], unit, False)
-    pl.semaphore_wait(barrier, 1 + len(bits))
-    for turn in (0, 1):
+    def receive(i, h):
+        query(i, h).wait_recv()
+        relay(i, h)
+
+    def expand(i, h):
+        right[i, pl.ds(h * part, part)] = augmented(q_in[i - 1, h], unit, False)
+
+    def answer(i, partial):
+        r_out[i - 1] = partial
+        result(i).start()
+
+    pl.semaphore_wait(barrier, 1 + 2 * len(bits))
+    for turn in range(parts):
         for bit in bits:
             query(bit, nth(bit, turn)).start()
     for copy in across:
         copy.start()
-    total = product(0)
+    prepare(0)
+    right[0] = augmented(p_data[0, mine], unit, False)
+    evaluate(right[0], 0, 0)
     for copy in across:
         copy.wait()
     prepare(1)
-    total += product(1)
+    evaluate(right[0], 1, 1)
+    total = product(0, 0) + product(1, 1)
+
+    near, far = 1, chips // 2
+    half = piece // 2
+    for turn in range(parts):
+        for bit in bits:
+            receive(bit, nth(bit, turn))
+        if 2 * turn + 2 == parts:
+            for bit in bits:
+                for done in range(turn + 1):
+                    expand(bit, nth(bit, done))
+            mixed = jnp.concatenate([right[near, :half], right[far, half:]], axis=0)
+            evaluate(mixed, 0, 0)
+    for bit in bits:
+        for turn in range(parts // 2, parts):
+            expand(bit, nth(bit, turn))
+    mixed = jnp.concatenate([right[near, half:], right[far, :half]], axis=0)
+    evaluate(mixed, 0, 1)
+    first = product(0, 0)
+    evaluate(right[near], 1, 0)
+    second = product(0, 1)
+    answer(far, jnp.concatenate([second[:, half:], first[:, half:]], axis=1))
+    crossed = jnp.concatenate([first[:, :half], second[:, :half]], axis=1)
+    answer(near, crossed + product(1, 0))
 
     for count in range(1, len(bits) + 1):
-        level = [i for i in others if i.bit_count() == count]
+        level = [i for i in others if i.bit_count() == count and i not in (near, far)]
         for i in level:
-            query(i, nth(i, 0)).wait_recv()
-            relay(i, nth(i, 0))
-        for i in level:
-            query(i, nth(i, 1)).wait_recv()
-            relay(i, nth(i, 1))
-            both = jnp.concatenate([q_in[i - 1, 0], q_in[i - 1, 1]], axis=0)
-            right[...] = augmented(both, unit, False)
-            partial = product(1)
-            if 2 * i != chips:
-                partial += product(0)
-            r_out[i - 1] = partial
-            result(i).start()
+            if count > 1:
+                for turn in range(parts):
+                    receive(i, nth(i, turn))
+                for h in range(parts):
+                    expand(i, h)
+            evaluate(right[i], 0, 0)
+            evaluate(right[i], 1, 1)
+            answer(i, product(0, 0) + product(1, 1))
 
     for i in others:
-        for h in (0, 1):
+        for h in range(parts):
             query(i, h).wait_send()
         result(i).wait()
         total += r_in[i - 1]
@@ -189,13 +222,14 @@
     rows, features = points.shape
     columns = vectors.shape[1]
     piece = rows // layers
-    assert blocks == 2 * layers and chips & (chips - 1) == 0
+    assert blocks == 2 * layers and chips >= 4 and chips & (chips - 1) == 0
     tile = min(256, rows)
+    parts = 4
     hbm = pl.BlockSpec(memory_space=pl.ANY)
     dma = pltpu.SemaphoreType.DMA
     peers = chips - 1
     out = pl.pallas_call(
-        functools.partial(kernel, chips, layers, tile),
+        functools.partial(kernel, chips, layers, parts, tile),
         out_shape=pltpu.VMEM((columns, piece), F32),
         in_specs=[hbm] * 4,
         out_specs=pl.BlockSpec(memory_space=pltpu.VMEM),
@@ -204,17 +238,17 @@
             pltpu.VMEM((2, columns, rows), F32),
             pltpu.VMEM((1, features), F32),
             pltpu.VMEM((1, piece), F32),
-            pltpu.VMEM((peers, 2, piece // 2, features), F32),
+            pltpu.VMEM((peers, parts, piece // parts, features), F32),
             pltpu.VMEM((2, rows, 4 * features), BF16),
             pltpu.VMEM((2, 2 * columns, rows), BF16),
-            pltpu.VMEM((piece, 4 * features), BF16),
-            pltpu.VMEM((rows, piece), BF16),
-            pltpu.VMEM((rows, piece), BF16),
+            pltpu.VMEM((chips, piece, 4 * features), BF16),
+            pltpu.VMEM((2, rows, piece), BF16),
+            pltpu.VMEM((2, rows, piece), BF16),
             pltpu.VMEM((peers, columns, piece), F32),
             pltpu.VMEM((peers, columns, piece), F32),
             dma((4,)),
             *[dma(()) for _ in range(4)],
-            *[dma((peers, 2)) for _ in range(2)],
+            *[dma((peers, parts)) for _ in range(2)],
             *[dma((peers,)) for _ in range(2)],
         ],
         compiler_params=pltpu.CompilerParams(collective_id=0, has_side_effects=True),

time: 18.1 us -> 15.9 us (0.88)
  the two profiles are of different devices: /device:TPU:0 before, /device:TPU:1 now
where the time goes in v3:
time: 15.9 us; the launch traced here: 15.7 us
  Pallas kernels  15.1 us (95%)
  local copies, waits for them, and re-layouts  0.63 us (4%)
    pallas_call x1, Pallas kernels, per_device(): pl.pallas_call(functools.partial(kernel, chips, layers, parts, tile), out...  15.1 us
    unnamed x1, local copies, waits for them, and re-layouts  0.63 us

profile of v3, /device:TPU:1, one launch (start us, length us, event | category | flops | bytes accessed | tf_op | source)
XLA Modules:
  0.0 15.7 jit_solution(5400216679977500443)
XLA Ops:
  0.0 15.1 %shard_map.46 = f32[64,256]{1,0:T(8,128)S(1)} custom-call(f32[1024,128]{1,0:T(8,128)} %points.1, f32[1,128]{1,0:T(1,128)} %bitcast.7, f32[64,1024]{1,0:T(8,128)} %bitcast.5, f32[1,256]{1,0:T(1,128)} %bitcast.6), custom_call_target="tpu_custom_call" | custom-call | tf_op jit(solution)/shard_map/pallas_call | solution.py:231
  15.1 0.6 %copy.6 = f32[256,64]{0,1:T(8,128)} copy(f32[256,64]{0,1:T(8,128)S(1)} %bitcast.4) | data formatting | bytes 131072

commit v4 on v3

--- a/solution.py
+++ b/solution.py
@@ -59,7 +59,7 @@
 
 def kernel(
     chips, layers, parts, tile, points, scale, vectors, noise, out,
-    p_data, v_data, s_data, n_data, q_in, left, v_left, right, high, low, r_out, r_in,
+    p_data, v_data, s_data, n_data, q_in, left, v_left, right, high, low, r_out, r_in, summed,
     own_sem, p_send, p_recv, v_send, v_recv, q_send, q_recv, r_send, r_recv,
 ):
     block, layer = lax.axis_index("blk"), lax.axis_index("layer")
@@ -156,6 +156,23 @@
         r_out[i - 1] = partial
         result(i).start()
 
+    near, far = 1, chips // 2
+    half = piece // 2
+    rest = [i for i in others if i not in (near, far)]
+    is_last = chip == chips - 1
+
+    def turns(first, last):
+        for turn in range(first, last):
+            for bit in bits:
+                receive(bit, nth(bit, turn))
+
+    def own_second():
+        summed[...] += product(1, 3)
+
+    def answer_far(first, second):
+        answer(far, jnp.concatenate([second[:, half:], first[:, half:]], axis=1))
+        r_out[near - 1] = jnp.concatenate([first[:, :half], second[:, :half]], axis=1)
+
     pl.semaphore_wait(barrier, 1 + 2 * len(bits))
     for turn in range(parts):
         for bit in bits:
@@ -165,55 +182,84 @@
     prepare(0)
     right[0] = augmented(p_data[0, mine], unit, False)
     evaluate(right[0], 0, 0)
+    summed[...] = product(0, 0)
     for copy in across:
         copy.wait()
     prepare(1)
-    evaluate(right[0], 1, 1)
-    total = product(0, 0) + product(1, 1)
-
-    near, far = 1, chips // 2
-    half = piece // 2
-    for turn in range(parts):
-        for bit in bits:
-            receive(bit, nth(bit, turn))
-        if 2 * turn + 2 == parts:
-            for bit in bits:
-                for done in range(turn + 1):
-                    expand(bit, nth(bit, done))
-            mixed = jnp.concatenate([right[near, :half], right[far, half:]], axis=0)
-            evaluate(mixed, 0, 0)
+
+    @pl.when(core == 0)
+    def _():
+        turns(0, parts // 2)
+
+    evaluate(right[0], 1, 3)
+
+    @pl.when(core == 1)
+    def _():
+        own_second()
+        turns(0, parts // 2)
+
+    for bit in bits:
+        for turn in range(parts // 2):
+            expand(bit, nth(bit, turn))
+    mixed = jnp.concatenate([right[near, :half], right[far, half:]], axis=0)
+    evaluate(mixed, 0, 0)
+    turns(parts // 2, parts)
     for bit in bits:
         for turn in range(parts // 2, parts):
             expand(bit, nth(bit, turn))
     mixed = jnp.concatenate([right[near, half:], right[far, :half]], axis=0)
-    evaluate(mixed, 0, 1)
-    first = product(0, 0)
-    evaluate(right[near], 1, 0)
-    second = product(0, 1)
-    answer(far, jnp.concatenate([second[:, half:], first[:, half:]], axis=1))
-    crossed = jnp.concatenate([first[:, :half], second[:, :half]], axis=1)
-    answer(near, crossed + product(1, 0))
-
-    for count in range(1, len(bits) + 1):
-        level = [i for i in others if i.bit_count() == count and i not in (near, far)]
-        for i in level:
-            if count > 1:
-                for turn in range(parts):
-                    receive(i, nth(i, turn))
-                for h in range(parts):
-                    expand(i, h)
-            evaluate(right[i], 0, 0)
-            evaluate(right[i], 1, 1)
-            answer(i, product(0, 0) + product(1, 1))
-
+
+    @pl.when(jnp.logical_not(is_last))
+    def _():
+        evaluate(mixed, 0, 1)
+        first = product(0, 0)
+        evaluate(right[near], 1, 2)
+        answer_far(first, product(0, 1))
+        answer(near, r_out[near - 1] + product(1, 2))
+
+    @pl.when(is_last)
+    def _():
+        evaluate(mixed, 0, 1)
+        first = product(0, 0)
+        answer_far(first, product(0, 1))
+
+    pl.when(core == 0)(own_second)
+    for i in sorted(rest, key=int.bit_count):
+        if i not in bits:
+            for turn in range(parts):
+                receive(i, nth(i, turn))
+            for h in range(parts):
+                expand(i, h)
+        evaluate(right[i], 0, 0)
+        evaluate(right[i], 1, 1)
+        answer(i, product(0, 0) + product(1, 1))
+
+    @pl.when(is_last)
+    def _():
+        evaluate(right[near], 1, 2)
+        r_out[near - 1] += product(1, 2)
+        for i in rest:
+            result(i).wait_send()
+        result(near).start()
+
+    normalizer = GAIN * float(rows * (2 * layers - 1)) ** (-0.5)
+    held = v_data[0, :, pl.ds(pl.multiple_of(layer * piece, 128), piece)]
+    gathered = summed[...] * normalizer + n_data[...] * held
+    for i in sorted(others, key=lambda i: (i.bit_count(), -i)):
+        result(i).wait_recv()
+        gathered += r_in[i - 1] * normalizer
+    out[...] = gathered
     for i in others:
         for h in range(parts):
             query(i, h).wait_send()
-        result(i).wait()
-        total += r_in[i - 1]
-    normalizer = GAIN * float(rows * (2 * layers - 1)) ** (-0.5)
-    held = v_data[0, :, pl.ds(pl.multiple_of(layer * piece, 128), piece)]
-    out[...] = total * normalizer + n_data[...] * held
+
+    @pl.when(jnp.logical_not(is_last))
+    def _():
+        for i in rest:
+            result(i).wait_send()
+
+    result(near).wait_send()
+    result(far).wait_send()
 
 
 def per_device(points, inv_scale, vectors, noise):
@@ -242,10 +288,11 @@
             pltpu.VMEM((2, rows, 4 * features), BF16),
             pltpu.VMEM((2, 2 * columns, rows), BF16),
             pltpu.VMEM((chips, piece, 4 * features), BF16),
-            pltpu.VMEM((2, rows, piece), BF16),
-            pltpu.VMEM((2, rows, piece), BF16),
+            pltpu.VMEM((4, rows, piece), BF16),
+            pltpu.VMEM((4, rows, piece), BF16),
             pltpu.VMEM((peers, columns, piece), F32),
             pltpu.VMEM((peers, columns, piece), F32),
+            pltpu.VMEM((columns, piece), F32),
             dma((4,)),
             *[dma(()) for _ in range(4)],
             *[dma((peers, parts)) for _ in range(2)],

time: 15.9 us -> 15.6 us (0.981)
  the two profiles are of different devices: /device:TPU:1 before, /device:TPU:0 now
where the time goes in v4:
time: 15.6 us; the launch traced here: 15.5 us
  Pallas kernels  14.8 us (95%)
  local copies, waits for them, and re-layouts  0.63 us (4%)
    pallas_call x1, Pallas kernels, per_device(): pl.pallas_call(functools.partial(kernel, chips, layers, parts, tile), out...  14.8 us
    unnamed x1, local copies, waits for them, and re-layouts  0.63 us

profile of v4, /device:TPU:0, one launch (start us, length us, event | category | flops | bytes accessed | tf_op | source)
XLA Modules:
  0.0 15.5 jit_solution(8491925638190731380)
XLA Ops:
  0.0 14.8 %shard_map.46 = f32[64,256]{1,0:T(8,128)S(1)} custom-call(f32[1024,128]{1,0:T(8,128)} %points.1, f32[1,128]{1,0:T(1,128)} %bitcast.7, f32[64,1024]{1,0:T(8,128)} %bitcast.5, f32[1,256]{1,0:T(1,128)} %bitcast.6), custom_call_target="tpu_custom_call" | custom-call | tf_op jit(solution)/shard_map/pallas_call | solution.py:277
  14.8 0.6 %copy.6 = f32[256,64]{0,1:T(8,128)} copy(f32[256,64]{0,1:T(8,128)S(1)} %bitcast.4) | data formatting | bytes 131072
